TPU v7x, 256 devices: a whole 4x4x8 slice. The times are simulated.
256 devices in a mesh: dp: 32 (over x, z_lo, core), head: 8 (over y, z_hi).
Axes of the slice: x: 4, y: 4, z: 8 (z_hi: 2, z_lo: 4; z = z_hi * 4 + z_lo), core: 2. Of those that a mesh axis runs over, the one named last changes fastest.
Arguments:
- frames_in: bfloat16 [32, 8, 320, 640], P('dp', 'head'), may hold values from -6 to 6
- ln1_gain: float32 [1280], replicated, may hold values from 0.25 to 1.75
- ln1_bias: float32 [1280], replicated, may hold values from -3 to 3
- qkv_weight: bfloat16 [1280, 3, 1024], P('dp', None, 'head'), may hold values from -0.1875 to 0.1875
- qv_bias: float32 [2, 1024], P(None, 'head'), may hold values from -3 to 3
- out_weight: bfloat16 [1024, 1280], P(('head', 'dp')), may hold values from -0.1875 to 0.1875
- out_bias: float32 [1280], P('head'), may hold values from -3 to 3
- ln2_gain: float32 [1280], replicated, may hold values from 0.25 to 1.75
- ln2_bias: float32 [1280], replicated, may hold values from -3 to 3
- fc1_weight: bfloat16 [1280, 5120], P('dp', 'head'), may hold values from -0.15625 to 0.15625
- fc1_bias: float32 [5120], P('head'), may hold values from -3 to 3
- fc2_weight: bfloat16 [5120, 1280], P(('head', 'dp')), may hold values from -0.078125 to 0.078125
- fc2_bias: float32 [1280], P('head'), may hold values from -3 to 3
- server_of_clip: int32 [32], replicated, may hold values from 0 to 7
Outputs:
- encoded: bfloat16 [32, 8, 320, 640], P('dp', 'head')
All inputs are finite; a program needn't handle non-finite values.
Results may differ from a plain program's by a relative error of at most 0.014.
Values may be sent and summed in bfloat16 or wider, within the bound.
No kernel may reach another device: no remote copies, remote signals or barrier semaphores. Data moves between devices by JAX's collectives and lax.ppermute only.
A program may use at most 64 MiB of HBM per device.

v0:
```python
import jax
import jax.numpy as jnp
from jax import lax
from jax.sharding import Mesh
from jax.sharding import PartitionSpec as P

HDIM = 64
HEAD = ("head_0", "head_1")
HEAD_DP = ("head_0", "head_1", "dp")


epsilon = 1e-05


def laid_out(blocks, dim):
    dims = list(blocks.shape[1:])
    dims[dim] *= blocks.shape[0]
    return jnp.moveaxis(blocks, 0, dim).reshape(dims)


def sent_to_all(value, axis):
    copies = jnp.broadcast_to(value, (lax.axis_size(axis), *value.shape))
    return lax.all_to_all(copies, axis, split_axis=0, concat_axis=0, tiled=True)


def gather_directly(value, axis, dim):
    return laid_out(sent_to_all(value, axis), dim)


def own_rows(terms, axes):
    total = terms.astype(jnp.bfloat16)
    for axis in axes:
        total = lax.psum_scatter(total, axis, scatter_dimension=0, tiled=True)
    return total.astype(jnp.float32)


def layer_norm(matrix, gain_row, shift_row):
    floats = matrix.astype(jnp.float32)
    center = jnp.mean(floats, axis=-1, keepdims=True)
    spread = jnp.mean(jnp.square(floats - center), axis=-1, keepdims=True)
    return ((floats - center) * lax.rsqrt(spread + epsilon) * gain_row + shift_row).astype(
        jnp.bfloat16
    )


def normalize(residual_in, gain_row, shift_row):
    whole_rows = lax.all_gather(residual_in, HEAD, axis=1, tiled=True)
    return layer_norm(whole_rows, gain_row, shift_row)


def attend(queries, key_rows, value_rows):

    def single(triple):
        query_head, key_head, value_head = triple
        scores = jnp.dot(query_head, key_head.T, preferred_element_type=jnp.float32)
        maxima = jnp.max(scores, axis=-1, keepdims=True)
        weights = jnp.exp(scores - maxima)
        probability = (weights / jnp.sum(weights, axis=-1, keepdims=True)).astype(jnp.bfloat16)
        return jnp.dot(probability, value_head, preferred_element_type=jnp.float32).astype(
            jnp.bfloat16
        )

    per_head = lax.map(
        single,
        (jnp.swapaxes(queries, 0, 1), jnp.swapaxes(key_rows, 0, 1), jnp.swapaxes(value_rows, 0, 1)),
    )
    return jnp.swapaxes(per_head, 0, 1).reshape(queries.shape[0], -1)


def slot_order(server_list):
    clip_count = server_list.shape[0]
    indices = jnp.arange(clip_count, dtype=jnp.int32)
    earlier = (server_list[None, :] < server_list[:, None]) | (
        server_list[None, :] == server_list[:, None]
    ) & (indices[None, :] < indices[:, None])
    slot_of = jnp.sum(earlier.astype(jnp.int32), axis=1)
    return jnp.sum(jnp.where(slot_of[None, :] == indices[:, None], indices[None, :], 0), axis=1)


def regroup(block_rows, clip_order):
    group_size = lax.axis_size("dp")
    piece_rows = block_rows.reshape(group_size, -1)
    shuffled = lax.all_to_all(piece_rows, "dp", split_axis=0, concat_axis=0, tiled=True)
    picked = jnp.take(shuffled, clip_order, axis=0)
    returned = lax.all_to_all(picked, "dp", split_axis=0, concat_axis=0, tiled=True)
    return returned.reshape(block_rows.shape)


def block_term(operand, weight_rows, row_count, frame_count, local_width):
    blocks = row_count // frame_count
    product = jnp.dot(operand, weight_rows, preferred_element_type=jnp.float32)
    return (
        product.reshape(frame_count, blocks, local_width)
        .transpose(1, 0, 2)
        .reshape(blocks * frame_count, local_width)
    )


def on_device(
    frames_in,
    ln1_gain,
    ln1_bias,
    qkv_weight,
    qv_bias,
    out_weight,
    out_bias,
    ln2_gain,
    ln2_bias,
    fc1_weight,
    fc1_bias,
    fc2_weight,
    fc2_bias,
    server_of_clip,
):
    clip_order = slot_order(server_of_clip)
    group_rows = frames_in.shape[2]
    local_width = frames_in.shape[3] // 4
    frame_count = group_rows * 4
    residual_in = frames_in[0, 0].reshape(frame_count, local_width)
    residual_in = regroup(residual_in, clip_order)
    head_count = lax.axis_size(HEAD)
    normed_one = normalize(residual_in, ln1_gain, ln1_bias)
    column_count = qkv_weight.shape[2]
    weight_piece = lax.all_gather(qkv_weight, "dp", axis=0, tiled=True)
    operand = normed_one
    projected = jnp.dot(
        operand, weight_piece.reshape(weight_piece.shape[0], -1), preferred_element_type=jnp.float32
    ).reshape(frame_count, 3, column_count)
    queries = (
        ((projected[:, 0] + qv_bias[0]) * HDIM ** (-0.5))
        .astype(jnp.bfloat16)
        .reshape(frame_count, -1, HDIM)
    )
    key_rows = projected[:, 1].astype(jnp.bfloat16).reshape(frame_count, -1, HDIM)
    value_rows = (projected[:, 2] + qv_bias[1]).astype(jnp.bfloat16).reshape(frame_count, -1, HDIM)
    context = attend(queries, key_rows, value_rows)
    output_rows = lax.all_gather(out_weight, "dp", axis=0, tiled=True)
    carried = residual_in.astype(jnp.float32) + out_bias
    whole_context = gather_directly(context, HEAD, 1)
    split_rows = output_rows.reshape(output_rows.shape[0], head_count, local_width)
    feature_columns = lax.all_to_all(
        split_rows, HEAD, split_axis=1, concat_axis=0, tiled=True
    ).reshape(-1, local_width)
    attended = (
        carried + jnp.dot(whole_context, feature_columns, preferred_element_type=jnp.float32)
    ).astype(jnp.bfloat16)
    normed_two = normalize(attended, ln2_gain, ln2_bias)
    operand = normed_two
    hidden_sums = jnp.dot(
        operand, gather_directly(fc1_weight, "dp", 0), preferred_element_type=jnp.float32
    )
    hidden = jax.nn.gelu(hidden_sums + fc1_bias, approximate=False).astype(jnp.bfloat16)
    down_rows = lax.all_gather(fc2_weight, "dp", axis=0, tiled=True)
    kept = attended.astype(jnp.float32) + fc2_bias
    layer_out = (
        kept
        + own_rows(
            block_term(
                hidden, down_rows, frame_count * lax.axis_size(HEAD), frame_count, local_width
            ),
            HEAD,
        )
    ).astype(jnp.bfloat16)
    return layer_out.reshape(1, 1, group_rows, 4 * local_width)


def solution(mesh):
    torus = Mesh(mesh.devices.reshape(mesh.shape["dp"], 4, 2), ("dp", "head_0", "head_1"))
    return jax.shard_map(
        on_device,
        mesh=torus,
        in_specs=(
            P("dp", HEAD, None, None),
            P(),
            P(),
            P("dp", None, HEAD),
            P(None, HEAD),
            P(HEAD_DP, None),
            P(HEAD),
            P(),
            P(),
            P("dp", HEAD),
            P(HEAD),
            P(HEAD_DP, None),
            P(HEAD),
            P(),
        ),
        out_specs=P("dp", HEAD, None, None),
        check_vma=False,
    )
```

profile of v0, /device:TPU:2, one launch (start us, length us, event | category | flops | bytes accessed | tf_op | source)
XLA Modules:
  0.0 520.5 jit_solution(1292017763583869009)
XLA Ops:
  7.4 2.4 all_to_all.38
  10.3 3.1 reduce.9
  14.3 9.1 %all-to-all-start = ((bf16[32,2,3200]{2,1,0:T(2,128)(2,1)}), bf16[32,2,3200]{2,1,0:T(2,128)(2,1)S(1)}, u32[]{:S(2)}, u32[]{:S(2)}) async-start(bf16[32,2,3200]{2,1,0:T(2,128)(2,1)} %reshape.166), calls=%async_computation | async-start | bytes 819200 | tf_op jit(solution)/shard_map/all_to_all | solution.py:83
  23.7 11.2 %all-to-all-done = bf16[32,2,3200]{2,1,0:T(2,128)(2,1)S(1)} async-done(((bf16[32,2,3200]{2,1,0:T(2,128)(2,1)}), bf16[32,2,3200]{2,1,0:T(2,128)(2,1)S(1)}, u32[]{:S(2)}, u32[]{:S(2)}) %all-to-all-start) | async-done | bytes 409632 | tf_op jit(solution)/shard_map/all_to_all | solution.py:83
  37.2 17.8 %all_to_all.44 = bf16[32,2,3200]{2,1,0:T(2,128)(2,1)S(1)} all-to-all(bf16[32,2,3200]{2,1,0:T(2,128)(2,1)S(1)} %reshape.168), channel_id=1, replica_groups=mesh['dp'=32,'head_0'=4,'head_1'=2] {'dp'}, dimensions={0} | all-to-all | bytes 819200 | tf_op jit(solution)/shard_map/all_to_all | solution.py:85
  55.4 2.4 reduce
  59.7 38.8 %all-gather = bf16[32,4,1280]{2,1,0:T(4,128)(2,1)S(1)} all-gather(bf16[1,4,1280]{2,1,0:T(4,128)(2,1)S(1)} %bitcast.96), channel_id=1, replica_groups=mesh['dp'=32,'head_0'=4,'head_1'=2] {'dp'}, dimensions={0}, use_global_device_ids=true | all-gather | bytes 337920 | tf_op jit(solution)/shard_map/all_gather | solution.py:137
  100.3 7.2 %all-to-all-start.3 = ((bf16[128,8,160]{0,2,1:T(8,128)(2,1)}), bf16[128,8,160]{0,2,1:T(8,128)(2,1)S(1)}, u32[]{:S(2)}, u32[]{:S(2)}) async-start(bf16[128,8,160]{0,2,1:T(8,128)(2,1)} %copy.63), calls=%async_computation.3 | async-start | bytes 655360 | tf_op jit(solution)/shard_map/all_to_all | solution.py:141
  107.5 64.5 %all_gather.16 = bf16[1280,3,128]{2,0,1:T(8,128)(2,1)S(1)} all-gather(bf16[40,3,128]{2,0,1:T(8,128)(2,1)S(1)} %copy-done.8), channel_id=1, replica_groups=mesh['dp'=32,'head_0'=4,'head_1'=2] {'dp'}, dimensions={0}, use_global_device_ids=true | all-gather | bytes 1013760 | tf_op jit(solution)/shard_map/all_gather | solution.py:124
  172.8 2.6 convert_reduce_fusion.1
  180.9 2.4 fusion.50
  183.3 8.4 %while.10 = (s32[]{:T(128)}, bf16[2,1280,64]{1,2,0:T(8,128)(2,1)}, bf16[2,1280,64]{2,1,0:T(8,128)(2,1)S(1)}, bf16[2,1280,64]{2,1,0:T(8,128)(2,1)S(1)}, bf16[2,1280,64]{2,1,0:T(8,128)(2,1)}, /*index=5*/s32[]{:T(128)}) while((s32[]{:T(128)}, bf16[2,1280,64]{1,2,0:T(8,128)(2,1)}, bf16[2,1280,64]{2,1,0:T(8,128)(2,1)S(1)}, ...), condition=%wide.region_7.8_spmd, body=%wide.region_4.7_spmd.sunk | while | flops 429340160 | bytes 24773784 | solution.py:63
  191.7 2.6 broadcast_in_dim.36
  194.4 8.3 %all-to-all-start.2 = ((bf16[8,1280,128]{1,2,0:T(8,128)(2,1)}), bf16[8,1280,128]{1,2,0:T(8,128)(2,1)S(1)}, u32[]{:S(2)}, u32[]{:S(2)}) async-start(bf16[8,1280,128]{1,2,0:T(8,128)(2,1)} %broadcast_in_dim.36), calls=%async_computation.2 | async-start | bytes 5242880 | tf_op jit(solution)/shard_map/all_to_all | solution.py:23
  204.2 61.5 %all-to-all-done.2 = bf16[8,1280,128]{1,2,0:T(8,128)(2,1)S(1)} async-done(((bf16[8,1280,128]{1,2,0:T(8,128)(2,1)}), bf16[8,1280,128]{1,2,0:T(8,128)(2,1)S(1)}, u32[]{:S(2)}, u32[]{:S(2)}) %all-to-all-start.2) | async-done | bytes 2621472 | tf_op jit(solution)/shard_map/all_to_all | solution.py:23
  269.5 12.5 %all-to-all-start.4 = ((bf16[32,40,640]{2,1,0:T(8,128)(2,1)}), bf16[32,40,640]{2,1,0:T(8,128)(2,1)}, u32[]{:S(2)}, u32[]{:S(2)}) async-start(bf16[32,40,640]{2,1,0:T(8,128)(2,1)} %broadcast_in_dim.37), calls=%async_computation.4 | async-start | bytes 3276800 | tf_op jit(solution)/shard_map/all_to_all | solution.py:23
  282.1 30.9 %all-gather.10.cloned.1.call-done = bf16[32,20,1280]{2,1,0:T(8,128)(2,1)} async-done(((bf16[1,20,1280]{2,1,0:T(8,128)(2,1)}), bf16[32,20,1280]{2,1,0:T(8,128)(2,1)}) %all-gather.10.cloned.1.call-update) | async-done | bytes 1638416 | tf_op jit(solution)/shard_map/all_gather | solution.py:153
  313.0 3.8 reshape.150
  316.8 95.9 %all-gather.8.cloned.1.call-done = bf16[1280,1280]{0,1:T(8,128)(2,1)} async-done(((bf16[1280,160]{0,1:T(8,128)(2,1)}), bf16[1280,1280]{0,1:T(8,128)(2,1)}) %all-gather.8.cloned.1.call-update) | async-done | bytes 3276816 | tf_op jit(solution)/shard_map/all_gather | solution.py:47
  412.7 2.6 convert_reduce_fusion
  416.6 15.6 %convolution_convert_fusion = bf16[1280,1280]{0,1:T(8,128)(2,1)} fusion(bf16[640,1280]{1,0:T(8,128)(2,1)} %reshape.150, bf16[1280,640]{1,0:T(8,128)(2,1)} %bitcast.24, bf16[1280,1280]{0,1:T(8,128)(2,1)S(1)} %copy-done.1, f32[1280]{0:T(1024)S(1)} %copy-done.15, f32[1280]{0:T(1024)S(1)} %copy-done.16, f32[1280]{0:T(1024)S(1)} %add_rsqrt_fusion, ...), kind=kOutput, calls=%fused_computation.25 | convolution fusion | flops 4259840000 | bytes 9853440 | tf_op jit(solution)/shard_map/dot_general | solution.py:91
  432.3 4.0 copy.71
  436.3 37.3 %reduce-scatter.3.cloned.1.call-done = bf16[2560,160]{0,1:T(8,128)(2,1)} async-done(((bf16[10240,160]{0,1:T(8,128)(2,1)}), bf16[2560,160]{0,1:T(8,128)(2,1)}) %reduce-scatter.3.cloned.1.call-update) | async-done | bytes 819216 | tf_op jit(solution)/shard_map/reduce_scatter | solution.py:33
  473.7 35.8 %reduce-scatter.5.cloned.1.call-done = bf16[1280,160]{0,1:T(8,128)(2,1)} async-done(((bf16[2560,160]{0,1:T(8,128)(2,1)}), bf16[1280,160]{0,1:T(8,128)(2,1)}) %reduce-scatter.5.cloned.1.call-update) | async-done | bytes 409616 | tf_op jit(solution)/shard_map/reduce_scatter | solution.py:33
  (104 shorter events, 32.2 us)
Async XLA Ops:
  7.4 16.0 %copy-start.18 = (s32[32]{0:T(128)S(1)}, s32[32]{0:T(128)}, u32[]{:S(2)}) copy-start(s32[32]{0:T(128)} %param.29) | copy-start | bytes 388
  14.3 20.7 %all-to-all-start = ((bf16[32,2,3200]{2,1,0:T(2,128)(2,1)}), bf16[32,2,3200]{2,1,0:T(2,128)(2,1)S(1)}, u32[]{:S(2)}, u32[]{:S(2)}) async-start(bf16[32,2,3200]{2,1,0:T(2,128)(2,1)} %reshape.166), calls=%async_computation | async-start | bytes 819200 | tf_op jit(solution)/shard_map/all_to_all | solution.py:83
  23.3 149.5 %all-gather.6.cloned.1.call-start = ((), (), s32[]{:S(2)}) async-start(), calls=%async_computation.7 | async-start | bytes 3686400 | tf_op jit(solution)/shard_map/all_gather | solution.py:47
  37.1 22.6 %copy-start.9 = (bf16[4,1280]{1,0:T(4,128)(2,1)S(1)}, bf16[4,1280]{1,0:T(4,128)(2,1)}, u32[]{:S(2)}) copy-start(bf16[4,1280]{1,0:T(4,128)(2,1)} %param.21) | copy-start | bytes 30724
  55.4 52.1 %copy-start.8 = (bf16[40,3,128]{2,0,1:T(8,128)(2,1)S(1)}, bf16[40,3,128]{2,0,1:T(8,128)(2,1)}, u32[]{:S(2)}) copy-start(bf16[40,3,128]{2,0,1:T(8,128)(2,1)} %param.19) | copy-start | bytes 92164
  59.7 113.0 %copy-start.10 = (f32[2,128]{1,0:T(2,128)S(1)}, f32[2,128]{1,0:T(2,128)}, u32[]{:S(2)}) copy-start(f32[2,128]{1,0:T(2,128)} %param.20) | copy-start | bytes 3076
  100.3 91.5 %all-to-all-start.3 = ((bf16[128,8,160]{0,2,1:T(8,128)(2,1)}), bf16[128,8,160]{0,2,1:T(8,128)(2,1)S(1)}, u32[]{:S(2)}, u32[]{:S(2)}) async-start(bf16[128,8,160]{0,2,1:T(8,128)(2,1)} %copy.63), calls=%async_computation.3 | async-start | bytes 655360 | tf_op jit(solution)/shard_map/all_to_all | solution.py:141
  172.8 3.9 copy-start.13
  172.8 3.9 copy-start.14
  172.8 2.9 copy-start
  194.4 71.4 %copy-start.2 = (bf16[1280,160]{0,1:T(8,128)(2,1)S(1)}, bf16[1280,160]{0,1:T(8,128)(2,1)}, u32[]{:S(2)}) copy-start(bf16[1280,160]{0,1:T(8,128)(2,1)} %copy.56) | copy-start | bytes 1228804
  194.4 71.4 %copy-start.12 = (f32[160]{0:T(256)S(1)}, f32[160]{0:T(256)}, u32[]{:S(2)}) copy-start(f32[160]{0:T(256)} %param.22) | copy-start | bytes 1924
  194.4 71.4 %all-to-all-start.2 = ((bf16[8,1280,128]{1,2,0:T(8,128)(2,1)}), bf16[8,1280,128]{1,2,0:T(8,128)(2,1)S(1)}, u32[]{:S(2)}, u32[]{:S(2)}) async-start(bf16[8,1280,128]{1,2,0:T(8,128)(2,1)} %broadcast_in_dim.36), calls=%async_computation.2 | async-start | bytes 5242880 | tf_op jit(solution)/shard_map/all_to_all | solution.py:23
  202.7 65.4 %copy-start.7 = (bf16[40,640]{1,0:T(8,128)(2,1)S(1)}, bf16[40,640]{1,0:T(8,128)(2,1)}, u32[]{:S(2)}) copy-start(bf16[40,640]{1,0:T(8,128)(2,1)} %param.25) | copy-start | bytes 153604
  202.7 110.3 %all-gather.10.cloned.1.call-start = ((), (), s32[]{:S(2)}) async-start(), calls=%async_computation.11 | async-start | bytes 2027520 | tf_op jit(solution)/shard_map/all_gather | solution.py:153
  203.3 209.4 %all-gather.8.cloned.1.call-start = ((), (), s32[]{:S(2)}) async-start(), calls=%async_computation.8 | async-start | bytes 3686400 | tf_op jit(solution)/shard_map/all_gather | solution.py:47
  269.5 147.1 %all-to-all-start.4 = ((bf16[32,40,640]{2,1,0:T(8,128)(2,1)}), bf16[32,40,640]{2,1,0:T(8,128)(2,1)}, u32[]{:S(2)}, u32[]{:S(2)}) async-start(bf16[32,40,640]{2,1,0:T(8,128)(2,1)} %broadcast_in_dim.37), calls=%async_computation.4 | async-start | bytes 3276800 | tf_op jit(solution)/shard_map/all_to_all | solution.py:23
  282.0 191.7 %reduce-scatter.3.cloned.1.call-start = ((), (), s32[]{:S(2)}) async-start(), calls=%async_computation.9 | async-start | bytes 4096000 | tf_op jit(solution)/shard_map/reduce_scatter | solution.py:33
  316.8 99.8 %copy-start.15 = (f32[1280]{0:T(1024)S(1)}, f32[1280]{0:T(1024)}, u32[]{:S(2)}) copy-start(f32[1280]{0:T(1024)} %param.24) | copy-start | bytes 15364
  316.8 99.8 %copy-start.16 = (f32[1280]{0:T(1024)S(1)}, f32[1280]{0:T(1024)}, u32[]{:S(2)}) copy-start(f32[1280]{0:T(1024)} %param.23) | copy-start | bytes 15364
  316.8 99.8 %copy-start.17 = (f32[640]{0:T(1024)S(1)}, f32[640]{0:T(1024)}, u32[]{:S(2)}) copy-start(f32[640]{0:T(1024)} %param.26) | copy-start | bytes 7684
  436.3 73.3 %copy-start.3 = (bf16[1280,160]{0,1:T(8,128)(2,1)S(1)}, bf16[1280,160]{0,1:T(8,128)(2,1)}, u32[]{:S(2)}) copy-start(bf16[1280,160]{0,1:T(8,128)(2,1)} %fusion.46) | copy-start | bytes 1228804
  436.3 73.3 %copy-start.11 = (f32[160]{0:T(256)S(1)}, f32[160]{0:T(256)}, u32[]{:S(2)}) copy-start(f32[160]{0:T(256)} %param.28) | copy-start | bytes 1924
  436.3 73.3 %reduce-scatter.5.cloned.1.call-start = ((), (), s32[]{:S(2)}) async-start(), calls=%async_computation.10 | async-start | bytes 1228800 | tf_op jit(solution)/shard_map/reduce_scatter | solution.py:33
  (7 other events, 8.9 us)
Sparse Core Ops, SparseCore 0:
  59.8 99.4 all-gather.5
  436.4 37.2 reduce-scatter.2
Sparse Core Ops, SparseCore 1:
  205.1 107.9 all-gather.9
  315.5 97.2 all-gather.7
  473.8 35.7 reduce-scatter.4
where the time goes:
time: 528 us; the launch traced here: 520 us
  waiting for transfers between devices  273 us (52%)
  blocking collectives  121 us (23%)
  starting transfers between devices  37.3 us (7%)
  local copies, waits for them, and re-layouts  29.2 us (6%)
  matrix products  24.4 us (5%)
  other arithmetic  19.4 us (4%)
  between operations  15.6 us (3%)
    all_gather x2, waiting for transfers between devices, normalize(): whole_rows = lax.all_gather(residual_in, HEAD, axis=1, tiled=True)  95.9 us
    reduce_scatter x2, waiting for transfers between devices, own_rows(): total = lax.psum_scatter(total, axis, scatter_dimension=0, tiled=True)  73.2 us
    all_gather x1, blocking collectives, on_device(): weight_piece = lax.all_gather(qkv_weight, 'dp', axis=0, tiled=True)  64.5 us
    all_to_all x2, waiting for transfers between devices, sent_to_all(): return lax.all_to_all(copies, axis, split_axis=0, concat_axis=0, tiled=True)  61.5 us
    all_gather x1, blocking collectives, on_device(): output_rows = lax.all_gather(out_weight, 'dp', axis=0, tiled=True)  38.8 us
    all_gather x1, waiting for transfers between devices, on_device(): down_rows = lax.all_gather(fc2_weight, 'dp', axis=0, tiled=True)  30.9 us
    all_to_all x2, starting transfers between devices, sent_to_all(): return lax.all_to_all(copies, axis, split_axis=0, concat_axis=0, tiled=True)  20.9 us
    all_to_all x1, blocking collectives, regroup(): lax.all_to_all(picked, 'dp', split_axis=0, concat_axis=0, tiled=True)  17.8 us
  transfers between devices with their start and end apart: 9, of which 6 were waited for; matrix products, arithmetic and copies ran while one was open for 6% of the time, Pallas kernels for 0%

commit v1 on v0

v1 whole, which is shorter than its diff:
```python
import jax
import jax.numpy as jnp
from jax import lax
from jax.sharding import Mesh
from jax.sharding import PartitionSpec as P

HDIM = 64
DP = ("x", "zl", "core")
HEAD = ("y", "zh")
EPS = 1e-05


def exchange(value, axes):
    return lax.all_to_all(value, axes, split_axis=0, concat_axis=0, tiled=True)


def gather_y(value):
    copies = jnp.broadcast_to(value[None], (4, *value.shape))
    return exchange(copies, "y").reshape(4 * value.shape[0], value.shape[1])


def norm_columns(matrix, gain, shift):
    floats = matrix.astype(jnp.float32)
    center = jnp.mean(floats, axis=0, keepdims=True)
    spread = jnp.mean(jnp.square(floats - center), axis=0, keepdims=True)
    return ((floats - center) * lax.rsqrt(spread + EPS) * gain[:, None] + shift[:, None]).astype(
        jnp.bfloat16
    )


def dot_rows(left, right):
    return lax.dot_general(
        left, right, (((0,), (0,)), ((), ())), preferred_element_type=jnp.float32
    )


def slot_order(server_list):
    clip_count = server_list.shape[0]
    indices = jnp.arange(clip_count, dtype=jnp.int32)
    earlier = (server_list[None, :] < server_list[:, None]) | (
        server_list[None, :] == server_list[:, None]
    ) & (indices[None, :] < indices[:, None])
    slot_of = jnp.sum(earlier.astype(jnp.int32), axis=1)
    return jnp.sum(jnp.where(slot_of[None, :] == indices[:, None], indices[None, :], 0), axis=1)


def attend(queries, key_rows, value_rows):
    outs = []
    for at in range(0, queries.shape[0], HDIM):
        scores = dot_rows(key_rows[at : at + HDIM], queries[at : at + HDIM])
        maxima = jnp.max(scores, axis=0, keepdims=True)
        weights = jnp.exp(scores - maxima)
        probs = (weights / jnp.sum(weights, axis=0, keepdims=True)).astype(jnp.bfloat16)
        outs.append(
            jnp.dot(
                value_rows[at : at + HDIM], probs, preferred_element_type=jnp.float32
            ).astype(jnp.bfloat16)
        )
    return jnp.concatenate(outs, axis=0)


def on_device(
    frames_in,
    ln1_gain,
    ln1_bias,
    qkv_weight,
    qv_bias,
    out_weight,
    out_bias,
    ln2_gain,
    ln2_bias,
    fc1_weight,
    fc1_bias,
    fc2_weight,
    fc2_bias,
    server_of_clip,
):
    bf16 = jnp.bfloat16
    y_at, core_at, zh_at = lax.axis_index("y"), lax.axis_index("core"), lax.axis_index("zh")

    plane = ("zh", "x", "zl", "core")
    w_qkv = lax.all_gather(qkv_weight.reshape(40, 384), plane, axis=0, tiled=True)
    w_out = lax.all_gather(out_weight, ("y",) + plane, axis=0, tiled=True)
    w_one = lax.all_gather(fc1_weight, plane, axis=0, tiled=True)
    w_two = lax.all_gather(fc2_weight, plane, axis=0, tiled=True)

    own = jnp.concatenate([qv_bias[0], qv_bias[1], fc1_bias, fc2_bias, out_bias])
    other = lax.ppermute(own, "zh", [(0, 1), (1, 0)])
    both = jnp.where(zh_at == 0, jnp.stack([own, other]), jnp.stack([other, own]))
    q_bias = both[:, 0:128].reshape(256, 1)
    v_bias = both[:, 128:256].reshape(256, 1)
    one_bias = both[:, 256:896].reshape(1280, 1)
    two_bias = both[:, 896:1056].reshape(320, 1)
    out_pair = both[:, 1056:1216].reshape(320)
    out_all = jnp.zeros((4, 320), jnp.float32)
    out_all = lax.dynamic_update_slice(out_all, out_pair[None], (y_at, 0))
    for step in (1, 2, 3):
        part = lax.ppermute(out_pair, "y", [(at, (at + step) % 4) for at in range(4)])
        out_all = lax.dynamic_update_slice(out_all, part[None], ((y_at - step) % 4, 0))
    out_all = out_all.reshape(1280, 1)

    clip_order = slot_order(server_of_clip)
    source_at = (clip_order % 2) * 16 + clip_order // 2
    source_at = source_at.reshape(16, 2).T.reshape(32)
    pieces = (
        frames_in[0, 0]
        .reshape(2, 160, 4, 160)
        .transpose(0, 3, 2, 1)
        .reshape(32, 10, 640)
    )
    shuffled = exchange(pieces, ("core", "x", "zl"))
    picked = jnp.take(shuffled, source_at, axis=0)
    block = exchange(picked, ("zh", "x", "zl")).reshape(320, 640)
    residual = gather_y(block)

    normed_one = norm_columns(residual, ln1_gain, ln1_bias)
    halves = [dot_rows(w_qkv[at : at + 1280], normed_one) for at in (0, 1280)]
    queries = jnp.concatenate([half[0:128] for half in halves], axis=0)
    queries = ((queries + q_bias) * HDIM ** (-0.5)).astype(bf16)
    keys = jnp.concatenate([half[128:256] for half in halves], axis=0).astype(bf16)
    values = jnp.concatenate([half[256:384] for half in halves], axis=0)
    values = (values + v_bias).astype(bf16)
    mine = jnp.concatenate([keys, values], axis=0)
    theirs = lax.ppermute(mine, "core", [(0, 1), (1, 0)])
    every = jnp.concatenate([mine, theirs], axis=1)
    context = attend(queries, every[:256], every[256:])

    whole_context = gather_y(context)
    attended = (
        residual.astype(jnp.float32) + out_all + dot_rows(w_out, whole_context)
    ).astype(bf16)
    normed_two = norm_columns(attended, ln2_gain, ln2_bias)
    sums = jnp.concatenate([dot_rows(w_one[at : at + 1280], normed_two) for at in (0, 1280)], axis=0)
    hidden = jax.nn.gelu(sums + one_bias, approximate=False).astype(bf16)
    terms = dot_rows(w_two, hidden).astype(bf16).reshape(4, 320, 640)
    arrived = exchange(terms, "y").astype(jnp.float32)
    kept = lax.dynamic_slice(attended, (y_at * 320, 0), (320, 640)).astype(jnp.float32)
    done = (kept + two_bias + jnp.sum(arrived, axis=0)).astype(bf16).reshape(2, 160, 640)

    same = [(j * 2 + k, k * 2 + j) for k in range(2) for j in range(2)]
    cross = [(j * 2 + k, k * 2 + 1 - j) for k in range(2) for j in range(2)]
    first = lax.ppermute(jnp.where(core_at == 0, done[0], done[1]), ("core", "zh"), same)
    second = lax.ppermute(jnp.where(core_at == 0, done[1], done[0]), ("core", "zh"), cross)
    halves = jnp.where(zh_at == 0, jnp.stack([first, second]), jnp.stack([second, first]))
    return halves.reshape(2, 160, 4, 160).transpose(0, 3, 2, 1).reshape(1, 1, 320, 640)


def solution(mesh):
    torus = Mesh(mesh.devices.reshape(4, 4, 2, 4, 2), ("x", "zl", "core", "y", "zh"))
    return jax.shard_map(
        on_device,
        mesh=torus,
        in_specs=(
            P(DP, HEAD, None, None),
            P(),
            P(),
            P(DP, None, HEAD),
            P(None, HEAD),
            P(HEAD + DP, None),
            P(HEAD),
            P(),
            P(),
            P(DP, HEAD),
            P(HEAD),
            P(HEAD + DP, None),
            P(HEAD),
            P(),
        ),
        out_specs=P(DP, HEAD, None, None),
        check_vma=False,
    )
```

time: 528 us -> 864 us (1.64)
  waiting for transfers between devices: 273 us -> 703 us
  blocking collectives: 121 us -> 29.4 us
  other arithmetic: 19.4 us -> 8.8 us
    all_gather x3 -> x4, waiting for transfers between devices: 127 us -> 616 us  [the longest x1 375 us: on_device(): w_out = lax.all_gather(out_weight, ('y',) + plane, axis=0, tiled=True)]
    all_gather x2 -> x0, blocking collectives: 103 us -> none  [the longest x1 64.5 us: on_device(): weight_piece = lax.all_gather(qkv_weight, 'dp', axis=0, tiled=True)]
    reduce_scatter x2 -> x0, waiting for transfers between devices: 73.2 us -> none  [own_rows(): total = lax.psum_scatter(total, axis, scatter_dimension=0, tiled=True)]
    ppermute x0 -> x7, waiting for transfers between devices: none -> 32.1 us  [the longest x1 12.9 us: on_device(): lax.ppermute(jnp.where(core_at == 0, done[1], done[0]), ('core', 'zh'), c...]
    all_to_all x4, waiting for transfers between devices: 72.8 us -> 52.6 us  [exchange(): return lax.all_to_all(value, axes, split_axis=0, concat_axis=0, tiled=True)]
    ppermute x0 -> x7, starting transfers between devices: none -> 15.7 us  [the longest x3 6.11 us: on_device(): lax.ppermute(out_pair, 'y', [(at, (at + step) % 4) for at in range(4)])]
    all_to_all x4, starting transfers between devices: 37.1 us -> 22.2 us  [exchange(): return lax.all_to_all(value, axes, split_axis=0, concat_axis=0, tiled=True)]
    all_to_all x1, blocking collectives: 17.8 us -> 29.4 us  [exchange(): return lax.all_to_all(value, axes, split_axis=0, concat_axis=0, tiled=True)]
  transfers between devices with their start and end apart: 9 -> 15, of which waited for: 6 -> 12; matrix products, arithmetic and copies ran while one was open for 6% -> 5% of each run, Pallas kernels for 0% -> 0%
where the time goes in v1:
time: 864 us; the launch traced here: 855 us
  waiting for transfers between devices  703 us (81%)
  starting transfers between devices  38 us (4%)
  matrix products  32.8 us (4%)
  blocking collectives  29.4 us (3%)
  local copies, waits for them, and re-layouts  29.2 us (3%)
  between operations  14 us (2%)
  other arithmetic  8.8 us (1%)
    all_gather x1, waiting for transfers between devices, on_device(): w_out = lax.all_gather(out_weight, ('y',) + plane, axis=0, tiled=True)  375 us
    all_gather x1, waiting for transfers between devices, on_device(): w_two = lax.all_gather(fc2_weight, plane, axis=0, tiled=True)  108 us
    all_gather x1, waiting for transfers between devices, on_device(): w_one = lax.all_gather(fc1_weight, plane, axis=0, tiled=True)  105 us
    all_to_all x4, waiting for transfers between devices, exchange(): return lax.all_to_all(value, axes, split_axis=0, concat_axis=0, tiled=True)  52.6 us
    dot_general x10, matrix products, dot_rows(): lax.dot_general(left, right, (((0,), (0,)), ((), ())), preferred_element_...  30.1 us
    all_to_all x1, blocking collectives, exchange(): return lax.all_to_all(value, axes, split_axis=0, concat_axis=0, tiled=True)  29.4 us
    all_gather x1, waiting for transfers between devices, on_device(): lax.all_gather(qkv_weight.reshape(40, 384), plane, axis=0, tiled=True)  28.3 us
    all_to_all x4, starting transfers between devices, exchange(): return lax.all_to_all(value, axes, split_axis=0, concat_axis=0, tiled=True)  22.2 us
  transfers between devices with their start and end apart: 15, of which 12 were waited for; matrix products, arithmetic and copies ran while one was open for 5% of the time, Pallas kernels for 0%

profile of v1, /device:TPU:2, one launch (start us, length us, event | category | flops | bytes accessed | tf_op | source)
XLA Modules:
  0.0 854.8 jit_solution(10657175189306649570)
XLA Ops:
  13.1 9.0 %all-to-all-start = ((bf16[32,10,640]{2,1,0:T(8,128)(2,1)}), bf16[32,10,640]{2,1,0:T(8,128)(2,1)S(1)}, u32[]{:S(2)}, u32[]{:S(2)}) async-start(bf16[32,10,640]{2,1,0:T(8,128)(2,1)} %reshape.133), calls=%async_computation | async-start | bytes 1310720 | tf_op jit(solution)/shard_map/all_to_all | solution.py:14
  22.8 17.5 %all-to-all-done = bf16[32,10,640]{2,1,0:T(8,128)(2,1)S(1)} async-done(((bf16[32,10,640]{2,1,0:T(8,128)(2,1)}), bf16[32,10,640]{2,1,0:T(8,128)(2,1)S(1)}, u32[]{:S(2)}, u32[]{:S(2)}) %all-to-all-start) | async-done | bytes 409632 | tf_op jit(solution)/shard_map/all_to_all | solution.py:14
  41.2 29.4 %all_to_all.25 = bf16[32,10,640]{2,1,0:T(8,128)(2,1)S(1)} all-to-all(bf16[32,10,640]{2,1,0:T(8,128)(2,1)S(1)} %broadcast_select_fusion), channel_id=1, replica_groups=mesh['x'=4,'zl'=4,'core'=2,'y'=4,'zh'=2] {'zh','x','zl'}, dimensions={0} | all-to-all | bytes 819200 | tf_op jit(solution)/shard_map/all_to_all | solution.py:14
  72.1 4.5 all-to-all-start.2
  79.4 5.0 collective-permute-done
  84.4 13.4 %all-to-all-done.2 = bf16[4,320,640]{2,1,0:T(8,128)(2,1)S(1)} async-done(((bf16[4,320,640]{2,1,0:T(8,128)(2,1)}), bf16[4,320,640]{2,1,0:T(8,128)(2,1)S(1)}, u32[]{:S(2)}, u32[]{:S(2)}) %all-to-all-start.2) | async-done | bytes 1638432 | tf_op jit(solution)/shard_map/all_to_all | solution.py:14
  99.2 28.3 %all-gather.7.cloned.1.call-done = bf16[2560,384]{1,0:T(8,128)(2,1)} async-done(((bf16[40,384]{1,0:T(8,128)(2,1)}), bf16[2560,384]{1,0:T(8,128)(2,1)}) %all-gather.7.cloned.1.call-update) | async-done | bytes 1966096 | tf_op jit(solution)/shard_map/all_gather | solution.py:82
  144.4 4.3 all-to-all-start.3
  155.1 8.6 %collective-permute-done.1 = f32[320]{0:T(512)S(1)} collective-permute-done((f32[320]{0:T(512)S(1)}, f32[320]{0:T(512)S(1)}, u32[]{:S(2)}, u32[]{:S(2)}) %collective-permute-start.1) | collective-permute-done | bytes 1312 | tf_op jit(solution)/shard_map/ppermute | solution.py:98
  163.8 3.6 collective-permute-done.2
  170.3 375.0 %all-gather.11.cloned.1.call-done = bf16[256,4,1280]{2,1,0:T(4,128)(2,1)} async-done(((bf16[1,4,1280]{2,1,0:T(4,128)(2,1)}), bf16[256,4,1280]{2,1,0:T(4,128)(2,1)}) %all-gather.11.cloned.1.call-update) | async-done | bytes 2621456 | tf_op jit(solution)/shard_map/all_gather | solution.py:83
  545.3 5.3 reshape.150
  550.6 4.2 convert_reduce_fusion
  556.7 104.8 %all-gather.9.cloned.1.call-done = bf16[2560,640]{1,0:T(8,128)(2,1)} async-done(((bf16[40,640]{1,0:T(8,128)(2,1)}), bf16[2560,640]{1,0:T(8,128)(2,1)}) %all-gather.9.cloned.1.call-update) | async-done | bytes 3276816 | tf_op jit(solution)/shard_map/all_gather | solution.py:84
  661.6 5.0 fusion.61
  666.5 2.9 fusion.64
  669.4 108.3 %all-gather.13.cloned.1.call-done = bf16[64,20,1280]{2,1,0:T(8,128)(2,1)} async-done(((bf16[1,20,1280]{2,1,0:T(8,128)(2,1)}), bf16[64,20,1280]{2,1,0:T(8,128)(2,1)}) %all-gather.13.cloned.1.call-update) | async-done | bytes 3276816 | tf_op jit(solution)/shard_map/all_gather | solution.py:85
  777.7 4.9 reshape.152
  782.6 12.1 %fusion.20 = bf16[1280,640]{0,1:T(8,128)(2,1)} fusion(bf16[1280,1280]{1,0:T(8,128)(2,1)S(1)} %reshape.152, f32[640,640]{1,0:T(8,128)} %fusion.64, f32[640,640]{1,0:T(8,128)} %fusion.61, f32[1280]{0:T(1024)S(1)} %add.183), kind=kOutput, calls=%fused_computation.47 | convolution fusion | flops 2152857600 | bytes 8197120 | tf_op jit(solution)/shard_map/dot_general | solution.py:32
  794.7 3.5 copy.38
  798.3 4.3 all-to-all-start.4
  802.6 21.7 %all-to-all-done.4 = bf16[4,320,640]{2,1,0:T(8,128)(2,1)S(1)} async-done(((bf16[4,320,640]{2,1,0:T(8,128)(2,1)}), bf16[4,320,640]{2,1,0:T(8,128)(2,1)S(1)}, u32[]{:S(2)}, u32[]{:S(2)}) %all-to-all-start.4) | async-done | bytes 1638432 | tf_op jit(solution)/shard_map/all_to_all | solution.py:14
  827.1 5.9 collective-permute-start.6
  833.0 12.9 %collective-permute-done.6 = bf16[160,640]{0,1:T(8,128)(2,1)S(1)} collective-permute-done((bf16[160,640]{0,1:T(8,128)(2,1)S(1)}, bf16[160,640]{0,1:T(8,128)(2,1)S(1)}, u32[]{:S(2)}, u32[]{:S(2)}) %collective-permute-start.6) | collective-permute-done | bytes 204832 | tf_op jit(solution)/shard_map/ppermute | solution.py:143
  (128 shorter events, 46.2 us)
Async XLA Ops:
  6.5 15.6 %copy-start.15 = (s32[32]{0:T(128)S(1)}, s32[32]{0:T(128)}, u32[]{:S(2)}) copy-start(s32[32]{0:T(128)} %param.27) | copy-start | bytes 388
  6.5 121.0 %all-gather.7.cloned.1.call-start = ((), (), s32[]{:S(2)}) async-start(), calls=%async_computation.5 | async-start | bytes 1996800 | tf_op jit(solution)/shard_map/all_gather | solution.py:82
  7.9 537.4 %all-gather.11.cloned.1.call-start = ((), (), s32[]{:S(2)}) async-start(), calls=%async_computation.7 | async-start | bytes 2631680 | tf_op jit(solution)/shard_map/all_gather | solution.py:83
  8.7 652.9 %all-gather.9.cloned.1.call-start = ((), (), s32[]{:S(2)}) async-start(), calls=%async_computation.6 | async-start | bytes 3328000 | tf_op jit(solution)/shard_map/all_gather | solution.py:84
  13.1 27.3 %all-to-all-start = ((bf16[32,10,640]{2,1,0:T(8,128)(2,1)}), bf16[32,10,640]{2,1,0:T(8,128)(2,1)S(1)}, u32[]{:S(2)}, u32[]{:S(2)}) async-start(bf16[32,10,640]{2,1,0:T(8,128)(2,1)} %reshape.133), calls=%async_computation | async-start | bytes 1310720 | tf_op jit(solution)/shard_map/all_to_all | solution.py:14
  70.6 6.1 copy-start.10
  72.1 26.5 %copy-start.5 = (f32[1280]{0:T(1024)S(1)}, f32[1280]{0:T(1024)}, u32[]{:S(2)}) copy-start(f32[1280]{0:T(1024)} %param.16) | copy-start | bytes 15364
  72.1 26.5 %copy-start.6 = (f32[1280]{0:T(1024)S(1)}, f32[1280]{0:T(1024)}, u32[]{:S(2)}) copy-start(f32[1280]{0:T(1024)} %param.15) | copy-start | bytes 15364
  72.1 25.7 %all-to-all-start.2 = ((bf16[4,320,640]{2,1,0:T(8,128)(2,1)}), bf16[4,320,640]{2,1,0:T(8,128)(2,1)S(1)}, u32[]{:S(2)}, u32[]{:S(2)}) async-start(bf16[4,320,640]{2,1,0:T(8,128)(2,1)} %broadcast_in_dim.38), calls=%async_computation.2 | async-start | bytes 3276800 | tf_op jit(solution)/shard_map/all_to_all | solution.py:14
  76.6 701.1 %all-gather.13.cloned.1.call-start = ((), (), s32[]{:S(2)}) async-start(), calls=%async_computation.8 | async-start | bytes 3993600 | tf_op jit(solution)/shard_map/all_gather | solution.py:85
  76.7 7.6 collective-permute-start
  132.0 2.6 collective-permute-start.4
  144.4 406.2 %all-to-all-start.3 = ((bf16[4,256,640]{2,1,0:T(8,128)(2,1)}), bf16[4,256,640]{2,1,0:T(8,128)(2,1)}, u32[]{:S(2)}, u32[]{:S(2)}) async-start(bf16[4,256,640]{2,1,0:T(8,128)(2,1)} %broadcast_in_dim.43), calls=%async_computation.3 | async-start | bytes 2621440 | tf_op jit(solution)/shard_map/all_to_all | solution.py:14
  148.9 14.8 %collective-permute-start.1 = (f32[320]{0:T(512)S(1)}, f32[320]{0:T(512)S(1)}, u32[]{:S(2)}, u32[]{:S(2)}) collective-permute-start(f32[320]{0:T(512)S(1)} %reshape.135), channel_id=1, source_target_pairs={{0,2},{2,4},{4,6},{6,0},{1,3},{3,5},{5,7},{7,1},{8,10},{10,12},{12... | collective-permute-start | bytes 3848 | tf_op jit(solution)/shard_map/ppermute | solution.py:98
  150.9 16.5 %collective-permute-start.2 = (f32[320]{0:T(512)S(1)}, f32[320]{0:T(512)S(1)}, u32[]{:S(2)}, u32[]{:S(2)}) collective-permute-start(f32[320]{0:T(512)S(1)} %reshape.135), channel_id=1, source_target_pairs={{0,4},{2,6},{4,0},{6,2},{1,5},{3,7},{5,1},{7,3},{8,12},{10,14},{12... | collective-permute-start | bytes 3848 | tf_op jit(solution)/shard_map/ppermute | solution.py:98
  153.5 13.9 %collective-permute-start.3 = (f32[320]{0:T(512)S(1)}, f32[320]{0:T(512)S(1)}, u32[]{:S(2)}, u32[]{:S(2)}) collective-permute-start(f32[320]{0:T(512)S(1)} %reshape.135), channel_id=1, source_target_pairs={{0,6},{2,0},{4,2},{6,4},{1,7},{3,1},{5,3},{7,5},{8,14},{10,8},{12,... | collective-permute-start | bytes 3848 | tf_op jit(solution)/shard_map/ppermute | solution.py:98
  170.3 380.3 %copy-start.2 = (f32[1280,640]{0,1:T(8,128)S(1)}, f32[1280,640]{0,1:T(8,128)}, u32[]{:S(2)}) copy-start(f32[1280,640]{0,1:T(8,128)} %copy.36) | copy-start | bytes 9830404
  550.6 111.0 %copy-start.13 = (f32[1280]{0:T(1024)S(1)}, f32[1280]{0:T(1024)}, u32[]{:S(2)}) copy-start(f32[1280]{0:T(1024)} %param.22) | copy-start | bytes 15364
  550.6 111.0 %copy-start.14 = (f32[1280]{0:T(1024)S(1)}, f32[1280]{0:T(1024)}, u32[]{:S(2)}) copy-start(f32[1280]{0:T(1024)} %param.21) | copy-start | bytes 15364
  556.7 109.8 %copy-start.4 = (bf16[1280,640]{0,1:T(8,128)(2,1)S(1)}, bf16[1280,640]{0,1:T(8,128)(2,1)}, u32[]{:S(2)}) copy-start(bf16[1280,640]{0,1:T(8,128)(2,1)} %copy-done.3) | copy-start | bytes 4915204
  798.3 26.1 %all-to-all-start.4 = ((bf16[4,320,640]{2,1,0:T(8,128)(2,1)}), bf16[4,320,640]{2,1,0:T(8,128)(2,1)S(1)}, u32[]{:S(2)}, u32[]{:S(2)}) async-start(bf16[4,320,640]{2,1,0:T(8,128)(2,1)} %bitcast.17), calls=%async_computation.4 | async-start | bytes 3276800 | tf_op jit(solution)/shard_map/all_to_all | solution.py:14
  824.6 23.3 %copy-start.1 = (bf16[40,3,128]{2,0,1:T(8,128)(2,1)S(1)}, bf16[40,3,128]{2,0,1:T(8,128)(2,1)}, u32[]{:S(2)}) copy-start(bf16[40,3,128]{2,0,1:T(8,128)(2,1)} %param.17) | copy-start | bytes 92164
  826.4 6.6 collective-permute-start.5
  827.1 18.8 %collective-permute-start.6 = (bf16[160,640]{0,1:T(8,128)(2,1)S(1)}, bf16[160,640]{0,1:T(8,128)(2,1)S(1)}, u32[]{:S(2)}, u32[]{:S(2)}) collective-permute-start(bf16[160,640]{0,1:T(8,128)(2,1)S(1)} %get-tuple-element.12), channel_id=1, source_target_pairs={{0,1},{8,0},{1,9},{9,8},{2,3},{10,2},{3,11},{11,10},{4,5},{12,4},{... | collective-permute-start | bytes 614408 | tf_op jit(solution)/shard_map/ppermute | solution.py:143
  (7 other events, 27.5 us)
Sparse Core Ops, SparseCore 0:
  9.2 118.2 all-gather.6
  129.4 415.8 all-gather.10
  547.2 114.3 all-gather.8
  663.3 114.3 all-gather.12
